TPU v7x, 256 devices: a whole 4x4x8 slice. The times are simulated.
256 devices in a mesh: row: 32 (over z, x_hi, core), col: 8 (over x_lo, y).
Axes of the slice: x: 4 (x_hi: 2, x_lo: 2; x = x_hi * 2 + x_lo), y: 4, z: 8, core: 2. Of those that a mesh axis runs over, the one named last changes fastest.
Arguments:
- counts: int32 [16384, 32768], P('row', 'col'), may hold values from 0 to 63
- row_support: int32 [16384], P(('row', 'col')), may hold values from 1 to 2209
- col_support: int32 [32768], P(('col', 'row')), may hold values from 1 to 2209
- total: int32 [1], replicated, may hold values from 256 to 4095
- sketch: bfloat16 [32768, 256], P('col'), may hold values from -6 to 6
Outputs:
- left_basis: float32 [16384, 256], P('row')
- right_basis: float32 [32768, 256], P('col')
All inputs are finite; a program needn't handle non-finite values.
Results may differ from a plain program's by a relative error of at most 0.012.
Values may be sent and summed in bfloat16 or wider, within the bound.
No kernel may reach another device: no remote copies, remote signals or barrier semaphores. Data moves between devices by JAX's collectives and lax.ppermute only.
A program may use at most 128 MiB of HBM per device.

v0:
```python
import jax
import jax.numpy as jnp
from jax import lax
from jax.sharding import Mesh
from jax.sharding import PartitionSpec as P

ROW = ("row_0", "row_1", "row_2")
ROW_COL = ("row_0", "row_1", "row_2", "col")
COL_ROW = ("col", "row_0", "row_1", "row_2")


def copy_for_each(shard, axis):
    count = lax.axis_size(axis)
    return lax.all_to_all(
        jnp.broadcast_to(shard[None], (count, *shard.shape)), axis, 0, 0, tiled=True
    )


def in_order(parts, dim):
    parts = jnp.moveaxis(parts, 0, dim)
    shape = parts.shape
    return parts.reshape(*shape[:dim], shape[dim] * shape[dim + 1], *shape[dim + 2 :])


def gather_directly(shard, axis, dim):
    parts = copy_for_each(shard, axis)
    return in_order(parts, dim)


def taken_together(shard, axis):
    return copy_for_each(shard, axis).sum(axis=0)


def split_up(shard, dim, count):
    before, after = (shard.shape[:dim], shard.shape[dim + 1 :])
    return jnp.moveaxis(shard.reshape(*before, count, -1, *after), dim, 0)


def sent_and_summed(shard, axis, dim):
    count = lax.axis_size(axis)
    parts = lax.all_to_all(split_up(shard, dim, count), axis, 0, 0, tiled=True)
    return jnp.sum(parts, axis=0)


def filled_up(lines, count):
    spare = -len(lines) % count
    return jnp.pad(lines, [(0, spare)] + [(0, 0)] * (lines.ndim - 1))


def sum_by_parts(shard, axes):
    lines = shard.reshape(-1, shard.shape[-1])
    own = sent_and_summed(filled_up(lines, lax.axis_size(axes)), axes, 0)
    whole = gather_directly(own, axes, 0)
    return whole[: len(lines)].reshape(shard.shape)


def gathered_by_axis(shard, axes, dim):
    far, near = axes
    leading = copy_for_each(shard, far)
    parts = jnp.swapaxes(copy_for_each(leading, near), 0, 1)
    return in_order(parts.reshape(-1, *shard.shape), dim)


def sum_by_axis(shard, axes, dim):
    far, near = axes
    own = sent_and_summed(split_up(shard, dim, lax.axis_size(far)), near, dim + 1)
    return jnp.sum(lax.all_to_all(own, far, 0, 0, tiled=True), axis=0)


def nested_sum(shard, axes):
    lines = shard.reshape(-1, shard.shape[-1])
    padded = filled_up(lines, lax.axis_size(axes[0]) * lax.axis_size(axes[1]))
    whole = gathered_by_axis(sum_by_axis(padded, axes, 0), axes, 0)
    return lax.slice_in_dim(whole, 0, len(lines)).reshape(shard.shape)


def lift(block, row_part, col_part, total):
    value = jnp.log(jnp.maximum(block, 1).astype(jnp.float32))
    value = value + jnp.log(total[0].astype(jnp.float32))
    value = value - jnp.log(row_part.astype(jnp.float32))[:, None]
    value = value - jnp.log(col_part.astype(jnp.float32))[None, :]
    return jnp.where(block > 0, jnp.maximum(value, 0.0), 0.0).astype(jnp.bfloat16)


def factor_of(gram):
    return jnp.linalg.cholesky(gram)


def solve_rows(lower, matrix):
    return jax.scipy.linalg.solve_triangular(lower, matrix.T, lower=True).T


def gram_of(matrix):
    return jnp.dot(matrix.T, matrix)


def per_device(counts, row_support, col_support, total, sketch):
    row_local = gather_directly(row_support, "col", 0)
    col_local = gather_directly(col_support, ROW, 0)
    table = lift(counts, row_local, col_local, total)
    row_count = table.shape[0]
    col_count = table.shape[1]

    def left_orth(rhs, narrow):
        whole = taken_together(jnp.dot(table, rhs, preferred_element_type=jnp.float32), "col")
        gram = sum_by_parts(gram_of(whole), ROW)
        basis = solve_rows(factor_of(gram), whole)
        if narrow:
            return basis.astype(jnp.bfloat16)
        return basis

    q_first = left_orth(sketch, True)
    partial_value = lax.dot_general(
        table, q_first, (((0,), (0,)), ((), ())), preferred_element_type=jnp.float32
    )
    whole = nested_sum(partial_value, (("row_0", "row_1"), "row_2"))
    gram = taken_together(gram_of(whole), "col")
    q_second = solve_rows(factor_of(gram), whole)
    q_third = left_orth(q_second.astype(jnp.bfloat16), False)
    total_rows = row_count * lax.axis_size(ROW)
    total_cols = col_count * lax.axis_size("col")
    return (
        q_third * jnp.sqrt(jnp.float32(total_rows)),
        q_second * jnp.sqrt(jnp.float32(total_cols)),
    )


def solution(mesh):
    split = Mesh(
        mesh.devices.reshape(8, 2, 2, mesh.shape["col"]), ("row_0", "row_1", "row_2", "col")
    )
    in_specs = (P(ROW, "col"), P(ROW_COL), P(COL_ROW), P(), P("col", None))
    out_specs = (P(ROW, None), P("col", None))
    return jax.shard_map(
        per_device, mesh=split, in_specs=in_specs, out_specs=out_specs, check_vma=False
    )
```

profile of v0, /device:TPU:1, one launch (start us, length us, event | category | flops | bytes accessed | tf_op | source)
XLA Modules:
  0.0 594.4 jit_solution(12490808932783963768)
XLA Ops:
  2.0 5.9 all-to-all-start
  14.2 12.9 %all-to-all-start.1 = ((s32[32,1,128]{2,1,0:T(1,128)}), s32[32,1,128]{2,1,0:T(1,128)S(1)}, u32[]{:S(2)}, u32[]{:S(2)}) async-start(s32[32,1,128]{2,1,0:T(1,128)} %broadcast_in_dim.22), calls=%async_computation.1 | async-start | bytes 32768 | tf_op jit(solution)/shard_map/all_to_all | solution.py:14
  27.2 9.2 %all-to-all-done.1 = s32[32,1,128]{2,1,0:T(1,128)S(1)} async-done(((s32[32,1,128]{2,1,0:T(1,128)}), s32[32,1,128]{2,1,0:T(1,128)S(1)}, u32[]{:S(2)}, u32[]{:S(2)}) %all-to-all-start.1) | async-done | bytes 16416 | tf_op jit(solution)/shard_map/all_to_all | solution.py:14
  36.4 5.5 select_convert_fusion
  47.5 4.5 all-to-all-start.2
  52.1 48.7 %all-to-all-done.2 = f32[8,512,256]{2,1,0:T(8,128)} async-done(((f32[8,512,256]{2,1,0:T(8,128)}), f32[8,512,256]{2,1,0:T(8,128)}, u32[]{:S(2)}, u32[]{:S(2)}) %all-to-all-start.2) | async-done | bytes 4194336 | tf_op jit(solution)/shard_map/all_to_all | solution.py:14
  103.7 16.4 %all_to_all.70 = f32[32,8,256]{2,1,0:T(8,128)S(1)} all-to-all(f32[32,8,256]{2,1,0:T(8,128)S(1)} %fusion.16), channel_id=1, replica_groups=mesh['row_0'=8,'row_1'=2,'row_2'=2,'col'=8] {'row_0','row_1','row_2'}, dimensions={0} | all-to-all | bytes 524288 | tf_op jit(solution)/shard_map/all_to_all | solution.py:41
  120.9 4.5 all-to-all-start.4
  125.3 12.8 %all-to-all-done.4 = f32[32,8,256]{2,1,0:T(8,128)S(1)} async-done(((f32[32,8,256]{2,1,0:T(8,128)}), f32[32,8,256]{2,1,0:T(8,128)S(1)}, u32[]{:S(2)}, u32[]{:S(2)}) %all-to-all-start.4) | async-done | bytes 262176 | tf_op jit(solution)/shard_map/all_to_all | solution.py:14
  138.3 11.7 %cholesky.172 = f32[128,128]{1,0:T(8,128)S(1)} custom-call(f32[128,128]{1,0:T(8,128)S(1)} %cholesky.270), custom_call_target="Cholesky" | custom-call | tf_op jit(solution)/shard_map/jit(cholesky)/cholesky | solution.py:86
  150.1 9.8 %custom-call.19 = f32[1,128,128]{1,2,0:T(8,128)S(1)} custom-call(f32[1,128,128]{2,1,0:T(8,128)S(1)} %get-tuple-element.77), custom_call_target="InvertDiagBlocksLowerTriangular" | custom-call | tf_op jit(solution)/shard_map/jit(cholesky)/cholesky | solution.py:86
  160.4 11.7 %cholesky.189 = f32[128,128]{1,0:T(8,128)S(1)} custom-call(f32[128,128]{1,0:T(8,128)S(1)} %convolution_subtract_fusion.5), custom_call_target="Cholesky" | custom-call | tf_op jit(solution)/shard_map/jit(cholesky)/cholesky | solution.py:86
  178.0 19.9 %custom-call.20 = f32[2,128,128]{1,2,0:T(8,128)S(1)} custom-call(f32[2,128,128]{2,1,0:T(8,128)S(1)} %get-tuple-element.26), custom_call_target="InvertDiagBlocksLowerTriangular" | custom-call | tf_op jit(solution)/shard_map/jit(_solve_triangular)/triangular_solve | solution.py:90
  203.0 8.2 %all_to_all.67 = f32[2,16,128,256]{3,2,1,0:T(8,128)} all-to-all(f32[2,16,128,256]{3,2,1,0:T(8,128)S(1)} %bitcast.172), channel_id=1, replica_groups=mesh['row_0'=8,'row_1'=2,'row_2'=2,'col'=8] {'row_2'}, dimensions={0} | all-to-all | bytes 8388608 | tf_op jit(solution)/shard_map/all_to_all | solution.py:41
  214.0 54.5 %all_to_all.71 = f32[16,128,256]{2,1,0:T(8,128)} all-to-all(f32[16,128,256]{2,1,0:T(8,128)S(1)} %reduce_sum.65), channel_id=1, replica_groups=mesh['row_0'=8,'row_1'=2,'row_2'=2,'col'=8] {'row_0','row_1'}, dimensions={0} | all-to-all | bytes 4194304 | tf_op jit(solution)/shard_map/all_to_all | solution.py:67
  270.4 55.1 %all_to_all.68 = f32[16,128,256]{2,1,0:T(8,128)S(1)} all-to-all(f32[16,128,256]{2,1,0:T(8,128)S(1)} %broadcast_in_dim.25), channel_id=1, replica_groups=mesh['row_0'=8,'row_1'=2,'row_2'=2,'col'=8] {'row_0','row_1'}, dimensions={0} | all-to-all | bytes 4194304 | tf_op jit(solution)/shard_map/all_to_all | solution.py:14
  326.0 9.3 %all_to_all.69 = f32[2,16,128,256]{3,2,1,0:T(8,128)S(1)} all-to-all(f32[2,16,128,256]{3,2,1,0:T(8,128)S(1)} %broadcast_in_dim.26), channel_id=1, replica_groups=mesh['row_0'=8,'row_1'=2,'row_2'=2,'col'=8] {'row_2'}, dimensions={0} | all-to-all | bytes 8388608 | tf_op jit(solution)/shard_map/all_to_all | solution.py:14
  343.5 4.6 copy.37
  348.2 5.6 copy.40
  353.8 15.9 %all-to-all-done.9 = f32[8,256,256]{2,1,0:T(8,128)S(1)} async-done(((f32[8,256,256]{2,1,0:T(8,128)}), f32[8,256,256]{2,1,0:T(8,128)S(1)}, u32[]{:S(2)}, u32[]{:S(2)}) %all-to-all-start.9) | async-done | bytes 2097184 | tf_op jit(solution)/shard_map/all_to_all | solution.py:14
  370.0 11.7 %cholesky.206 = f32[128,128]{1,0:T(8,128)S(1)} custom-call(f32[128,128]{1,0:T(8,128)S(1)} %cholesky.273), custom_call_target="Cholesky" | custom-call | tf_op jit(solution)/shard_map/jit(cholesky)/cholesky | solution.py:86
  382.4 9.8 %custom-call.21 = f32[1,128,128]{1,2,0:T(8,128)S(1)} custom-call(f32[1,128,128]{2,1,0:T(8,128)S(1)} %get-tuple-element.73), custom_call_target="InvertDiagBlocksLowerTriangular" | custom-call | tf_op jit(solution)/shard_map/jit(cholesky)/cholesky | solution.py:86
  392.8 11.7 %cholesky.223 = f32[128,128]{1,0:T(8,128)S(1)} custom-call(f32[128,128]{1,0:T(8,128)S(1)} %convolution_subtract_fusion.4), custom_call_target="Cholesky" | custom-call | tf_op jit(solution)/shard_map/jit(cholesky)/cholesky | solution.py:86
  410.3 19.8 %custom-call.15 = f32[2,128,128]{1,2,0:T(8,128)S(1)} custom-call(f32[2,128,128]{2,1,0:T(8,128)S(1)} %get-tuple-element.19), custom_call_target="InvertDiagBlocksLowerTriangular" | custom-call | tf_op jit(solution)/shard_map/jit(_solve_triangular)/triangular_solve | solution.py:90
  439.4 52.0 %all_to_all.72 = f32[8,512,256]{2,1,0:T(8,128)} all-to-all(f32[8,512,256]{2,1,0:T(8,128)S(1)} %broadcast_in_dim.28), channel_id=1, replica_groups=mesh['row_0'=8,'row_1'=2,'row_2'=2,'col'=8] {'col'}, dimensions={0} | all-to-all | bytes 8388608 | tf_op jit(solution)/shard_map/all_to_all | solution.py:14
  494.4 18.6 %all_to_all.73 = f32[32,8,256]{2,1,0:T(8,128)S(1)} all-to-all(f32[32,8,256]{2,1,0:T(8,128)S(1)} %fusion.14), channel_id=1, replica_groups=mesh['row_0'=8,'row_1'=2,'row_2'=2,'col'=8] {'row_0','row_1','row_2'}, dimensions={0} | all-to-all | bytes 524288 | tf_op jit(solution)/shard_map/all_to_all | solution.py:41
  513.8 4.4 all-to-all-start.12
  522.3 5.7 copy.44
  531.2 11.7 %cholesky.240 = f32[128,128]{1,0:T(8,128)S(1)} custom-call(f32[128,128]{1,0:T(8,128)S(1)} %cholesky.276), custom_call_target="Cholesky" | custom-call | tf_op jit(solution)/shard_map/jit(cholesky)/cholesky | solution.py:86
  543.6 9.8 %custom-call.22 = f32[1,128,128]{1,2,0:T(8,128)S(1)} custom-call(f32[1,128,128]{2,1,0:T(8,128)S(1)} %get-tuple-element.69), custom_call_target="InvertDiagBlocksLowerTriangular" | custom-call | tf_op jit(solution)/shard_map/jit(cholesky)/cholesky | solution.py:86
  553.9 11.7 %cholesky.257 = f32[128,128]{1,0:T(8,128)S(1)} custom-call(f32[128,128]{1,0:T(8,128)S(1)} %convolution_subtract_fusion.3), custom_call_target="Cholesky" | custom-call | tf_op jit(solution)/shard_map/jit(cholesky)/cholesky | solution.py:86
  571.9 19.9 %custom-call.23 = f32[2,128,128]{1,2,0:T(8,128)S(1)} custom-call(f32[2,128,128]{2,1,0:T(8,128)S(1)} %get-tuple-element.27), custom_call_target="InvertDiagBlocksLowerTriangular" | custom-call | tf_op jit(solution)/shard_map/jit(_solve_triangular)/triangular_solve | solution.py:90
  (115 shorter events, 86.4 us)
Async XLA Ops:
  0.6 43.3 %copy-start = (bf16[4096,256]{1,0:T(8,128)(2,1)S(1)}, bf16[4096,256]{1,0:T(8,128)(2,1)}, u32[]{:S(2)}) copy-start(bf16[4096,256]{1,0:T(8,128)(2,1)} %param.12) | copy-start | bytes 6291460
  2.0 10.9 %all-to-all-start = ((s32[8,1,64]{2,1,0:T(1,128)}), s32[8,1,64]{2,1,0:T(1,128)S(1)}, u32[]{:S(2)}, u32[]{:S(2)}) async-start(s32[8,1,64]{2,1,0:T(1,128)} %broadcast_in_dim.20), calls=%async_computation | async-start | bytes 8192 | tf_op jit(solution)/shard_map/all_to_all | solution.py:14
  14.2 22.2 %all-to-all-start.1 = ((s32[32,1,128]{2,1,0:T(1,128)}), s32[32,1,128]{2,1,0:T(1,128)S(1)}, u32[]{:S(2)}, u32[]{:S(2)}) async-start(s32[32,1,128]{2,1,0:T(1,128)} %broadcast_in_dim.22), calls=%async_computation.1 | async-start | bytes 32768 | tf_op jit(solution)/shard_map/all_to_all | solution.py:14
  41.9 2.0 copy-start.3
  47.5 53.2 %all-to-all-start.2 = ((f32[8,512,256]{2,1,0:T(8,128)}), f32[8,512,256]{2,1,0:T(8,128)}, u32[]{:S(2)}, u32[]{:S(2)}) async-start(f32[8,512,256]{2,1,0:T(8,128)} %broadcast_in_dim.23), calls=%async_computation.2 | async-start | bytes 8388608 | tf_op jit(solution)/shard_map/all_to_all | solution.py:14
  120.9 17.3 %all-to-all-start.4 = ((f32[32,8,256]{2,1,0:T(8,128)}), f32[32,8,256]{2,1,0:T(8,128)S(1)}, u32[]{:S(2)}, u32[]{:S(2)}) async-start(f32[32,8,256]{2,1,0:T(8,128)} %broadcast_in_dim.24), calls=%async_computation.4 | async-start | bytes 524288 | tf_op jit(solution)/shard_map/all_to_all | solution.py:14
  335.3 1.9 copy-start.2
  339.5 30.2 %all-to-all-start.9 = ((f32[8,256,256]{2,1,0:T(8,128)}), f32[8,256,256]{2,1,0:T(8,128)S(1)}, u32[]{:S(2)}, u32[]{:S(2)}) async-start(f32[8,256,256]{2,1,0:T(8,128)} %broadcast_in_dim.27), calls=%async_computation.9 | async-start | bytes 4194304 | tf_op jit(solution)/shard_map/all_to_all | solution.py:14
  430.2 3.7 copy-start.5
  433.9 3.9 copy-start.4
  437.8 1.3 copy-start.6
  513.8 17.3 %all-to-all-start.12 = ((f32[32,8,256]{2,1,0:T(8,128)}), f32[32,8,256]{2,1,0:T(8,128)S(1)}, u32[]{:S(2)}, u32[]{:S(2)}) async-start(f32[32,8,256]{2,1,0:T(8,128)} %broadcast_in_dim.29), calls=%async_computation.12 | async-start | bytes 524288 | tf_op jit(solution)/shard_map/all_to_all | solution.py:14
  522.3 71.8 %copy-start.1 = (bf16[4096,256]{1,0:T(8,128)(2,1)S(1)}, bf16[4096,256]{1,0:T(8,128)(2,1)}, u32[]{:S(2)}) copy-start(bf16[4096,256]{1,0:T(8,128)(2,1)} %param.12) | copy-start | bytes 6291460
where the time goes:
time: 600 us; the launch traced here: 594 us
  blocking collectives  214 us (36%)
  other arithmetic  182 us (30%)
  waiting for transfers between devices  93.8 us (16%)
  local copies, waits for them, and re-layouts  43.1 us (7%)
  starting transfers between devices  36.3 us (6%)
  matrix products  18.6 us (3%)
    all_to_all x3, blocking collectives, copy_for_each(): lax.all_to_all(jnp.broadcast_to(shard[None], (count, *shard.shape)), axis...  116 us
    another operation x20, other arithmetic, factor_of(): return jnp.linalg.cholesky(gram)  103 us
    all_to_all x6, waiting for transfers between devices, copy_for_each(): lax.all_to_all(jnp.broadcast_to(shard[None], (count, *shard.shape)), axis...  93.8 us
    another operation x7, other arithmetic, solve_rows(): return jax.scipy.linalg.solve_triangular(lower, matrix.T, lower=True).T  59.8 us
    all_to_all x1, blocking collectives, sum_by_axis(): return jnp.sum(lax.all_to_all(own, far, 0, 0, tiled=True), axis=0)  54.5 us
    all_to_all x3, blocking collectives, sent_and_summed(): parts = lax.all_to_all(split_up(shard, dim, count), axis, 0, 0, tiled=True)  43.2 us
    all_to_all x6, starting transfers between devices, copy_for_each(): lax.all_to_all(jnp.broadcast_to(shard[None], (count, *shard.shape)), axis...  36.3 us
  transfers between devices with their start and end apart: 6, of which 6 were waited for; matrix products, arithmetic and copies ran while one was open for 3% of the time, Pallas kernels for 0%

commit v1 on v0

v1 whole, which is shorter than its diff:
```python
import functools

import jax
import jax.numpy as jnp
from jax import lax
from jax.experimental import pallas as pl
from jax.experimental.pallas import tpu as pltpu
from jax.sharding import Mesh
from jax.sharding import PartitionSpec as P

PLANE = ("z", "far")
ROW = ("z", "far", "core")
F32 = jnp.float32
BF16 = jnp.bfloat16
EXACT = lax.Precision.HIGHEST
LEAD = 16
BLOCK = 32


def call(body, out_shape, *args, **options):
    return pl.pallas_call(
        body,
        out_shape=out_shape,
        compiler_params=pltpu.CompilerParams(vmem_limit_bytes=options.pop("vmem", 24) << 20),
        **options,
    )(*args)


def shaped(shape, dtype=F32):
    return jax.ShapeDtypeStruct(shape, dtype)


def exchange(parts, axes):
    return lax.all_to_all(parts, axes, 0, 0, tiled=True)


def copy_for_each(shard, axes):
    count = lax.axis_size(axes)
    return exchange(jnp.broadcast_to(shard[None], (count, *shard.shape)), axes)


def over_rows(left, right, precision=None):
    return lax.dot_general(
        left, right, (((0,), (0,)), ((), ())), precision=precision, preferred_element_type=F32
    )


def over_lanes(left, right, precision=None):
    return lax.dot_general(
        left, right, (((1,), (1,)), ((), ())), precision=precision, preferred_element_type=F32
    )


def lift_body(counts, rows, cols, total, sketch, table, part, acc):
    step = pl.program_id(0)
    base = jnp.log(total[...].astype(F32)) - jnp.log(rows[...].astype(F32))
    block = counts[...]
    value = jnp.log(jnp.maximum(block, 1).astype(F32))
    value = value + base
    value = value - jnp.log(cols[...].astype(F32))
    lifted = jnp.where(block > 0, jnp.maximum(value, 0.0), 0.0).astype(BF16)
    table[...] = lifted
    added = jnp.dot(lifted, sketch[...], preferred_element_type=F32)

    @pl.when(step == 0)
    def _():
        acc[...] = added

    @pl.when(step > 0)
    def _():
        acc[...] += added

    @pl.when(step == pl.num_programs(0) - 1)
    def _():
        part[...] = acc[...]


def lift(counts, rows, cols, total, sketch, wide=512):
    height, width = counts.shape
    rank = sketch.shape[1]
    return call(
        lift_body,
        (shaped((height, width), BF16), shaped((height, rank))),
        counts,
        rows.reshape(height, 1),
        cols.reshape(1, width),
        total.reshape(1, 1),
        sketch,
        grid=(width // wide,),
        in_specs=[
            pl.BlockSpec((height, wide), lambda i: (0, i)),
            pl.BlockSpec((height, 1), lambda i: (0, 0)),
            pl.BlockSpec((1, wide), lambda i: (0, i)),
            pl.BlockSpec((1, 1), lambda i: (0, 0)),
            pl.BlockSpec((wide, rank), lambda i: (i, 0)),
        ],
        out_specs=[
            pl.BlockSpec((height, wide), lambda i: (0, i)),
            pl.BlockSpec((height, rank), lambda i: (0, 0)),
        ],
        scratch_shapes=[pltpu.VMEM((height, rank), F32)],
    )


def summed(ref):
    value = ref[0].astype(F32)
    for i in range(1, ref.shape[0]):
        value = value + ref[i].astype(F32)
    return value


def spread_body(parts, out):
    value = summed(parts)
    for i in range(out.shape[0]):
        out[i] = value


def sum_and_spread(parts, count):
    return call(spread_body, shaped((count, *parts.shape[1:])), parts)


def diag_inverse(tile, lane0, size):
    groups = size // 8
    sub = lax.broadcasted_iota(jnp.int32, (8, 128), 0)
    lane = lax.broadcasted_iota(jnp.int32, (8, 128), 1)
    col = [
        {
            g: jnp.broadcast_to(tile[8 * g : 8 * g + 8, lane0 + j : lane0 + j + 1], (8, 128))
            for g in range(j // 8, groups)
        }
        for j in range(size)
    ]
    inv = [jnp.where(lane == sub + (lane0 + 8 * g), 1.0, 0.0).astype(F32) for g in range(groups)]
    scale = [jnp.zeros((8, 128), F32) for _ in range(groups)]

    def row(value, i):
        return jnp.broadcast_to(value[i : i + 1, :], (8, 128))

    for j in range(size):
        gj, sj = divmod(j, 8)
        root = lax.rsqrt(row(col[j][gj], sj))
        scale[gj] = jnp.where(sub == sj, root, scale[gj])
        over = root * root
        part = {g: col[j][g] * over for g in range(gj, groups)}
        part[gj] = jnp.where(sub > sj, part[gj], 0.0)
        for k in range(j + 1, size):
            pivot = row(col[j][k // 8], k % 8)
            for g in range(k // 8, groups):
                col[k][g] = col[k][g] - part[g] * pivot
        own = row(inv[gj], sj)
        for g in range(gj, groups):
            inv[g] = inv[g] - part[g] * own
    return jnp.concatenate([inv[g] * scale[g] for g in range(groups)], axis=0)


def invert_factor(m, size=BLOCK):
    n = m.shape[0]
    for r0 in range(0, n, size):
        t0 = r0 // 128 * 128
        inv = diag_inverse(m[r0 : r0 + size, t0 : t0 + 128], r0 - t0, size)
        rows = jnp.dot(inv, m[t0 : t0 + 128, :], precision=EXACT, preferred_element_type=F32)
        column = lax.broadcasted_iota(jnp.int32, (size, n), 1)
        wide = jnp.concatenate([inv if t == t0 else jnp.zeros_like(inv) for t in range(0, n, 128)], axis=1)
        done = jnp.where((column >= r0) & (column < r0 + size), wide, rows)
        m[r0 : r0 + size, :] = done
        if r0 + size < n:
            base = (r0 + size) // 128 * 128
            left = jnp.where(column >= r0 + size, rows, 0.0)[:, base:]
            change = over_rows(left, done, EXACT)
            below = m[r0 + size :, :]
            at = lax.broadcasted_iota(jnp.int32, below.shape, 1)
            below = jnp.where((at >= r0) & (at < r0 + size), 0.0, below)
            m[r0 + size :, :] = below - change[r0 + size - base :, :]
    i = lax.broadcasted_iota(jnp.int32, (n, n), 0)
    j = lax.broadcasted_iota(jnp.int32, (n, n), 1)
    return jnp.where(i >= j, m[...], 0.0)


def lead_change(gram):
    lead, rank = gram.shape
    inv = diag_inverse(gram[:, :128], 0, lead)[:, :lead]
    solved = over_rows(inv, jnp.dot(inv, gram, precision=EXACT, preferred_element_type=F32), EXACT)
    i = lax.broadcasted_iota(jnp.int32, (lead, rank), 0)
    j = lax.broadcasted_iota(jnp.int32, (lead, rank), 1)
    unit = jnp.where(i == j, 1.0, 0.0)
    size = jnp.sqrt(jnp.sum(jnp.sum(gram * unit, axis=1, keepdims=True), axis=0, keepdims=True) / lead)
    own = over_rows(inv, unit, EXACT) * size - unit
    return jnp.where(j < lead, own, -solved)


def lead_out(value, change):
    lead = change.shape[0]
    return value + jnp.dot(value[:, :lead], change, precision=EXACT, preferred_element_type=F32)


def lead_gram(value):
    return over_rows(value[:, :128], value, EXACT)[:LEAD, :]


def first_gram_body(value, out):
    gram = lead_gram(value[...])
    for i in range(out.shape[0]):
        out[i] = gram


def send_half_body(core, grams, value, table, first, out):
    cleared = lead_out(value[...], lead_change(summed(grams))).astype(BF16)
    first[...] = cleared
    half = out.shape[0]
    other = pl.multiple_of((1 - core[0]) * half, half)
    out[...] = over_rows(table[:, pl.ds(other, half)], cleared)


def keep_half_body(core, first, table, out):
    half = out.shape[0]
    mine = pl.multiple_of(core[0] * half, half)
    out[...] = over_rows(table[:, pl.ds(mine, half)], first[...])


def add_body(left, right, out):
    out[...] = (left[...] + right[...]).astype(BF16)


def second_gram_body(parts, piece, out):
    value = summed(parts)
    piece[...] = value
    gram = lead_gram(value)
    for i in range(out.shape[0]):
        out[i] = gram


def clear_body(grams, piece, out):
    value = lead_out(piece[...], lead_change(summed(grams))).astype(BF16)
    for i in range(out.shape[0]):
        out[i] = value


def third_body(core, mine, other, table, out):
    half = mine.shape[0]
    at = pl.multiple_of(core[0] * half, half)
    rest = pl.multiple_of((1 - core[0]) * half, half)
    own, far = mine[...], other[...]
    value = jnp.dot(table[:, pl.ds(at, half)], own, preferred_element_type=F32)
    value = value + jnp.dot(table[:, pl.ds(rest, half)], far, preferred_element_type=F32)
    gram = over_rows(own, own) + over_rows(far, far)
    count = out.shape[0]
    deep, thin = value.shape[0] // count, gram.shape[0] // count
    for i in range(count):
        out[i, :deep, :] = value[i * deep : (i + 1) * deep, :]
        out[i, deep:, :] = gram[i * thin : (i + 1) * thin, :]


def third_gram_body(value, out):
    out[...] = over_rows(value[...], value[...], EXACT)


def split(value):
    high = value.astype(BF16)
    return high, (value - high.astype(F32)).astype(BF16)


def last_body(root_left, root_right, core, second, third, mine, other, value, left, right, work, work2):
    work[...] = third[...]
    work2[...] = second[...]
    inverse = invert_factor(work2)
    high, low = split(inverse * root_right)
    half = mine.shape[0]
    for source, at in ((mine, core[0]), (other, 1 - core[0])):
        start = pl.multiple_of(at * half, half)
        right[pl.ds(start, half), :] = over_lanes(source[...], high) + over_lanes(source[...], low)
    left[...] = over_lanes(value[...], invert_factor(work) * root_left, EXACT)


VM = pl.BlockSpec(memory_space=pltpu.VMEM)
SM = pl.BlockSpec(memory_space=pltpu.SMEM)


def per_device(counts, row_support, col_support, total, sketch):
    rows, cols, planes = lax.axis_size(ROW), lax.axis_size("col"), lax.axis_size(PLANE)
    core = lax.axis_index("core").reshape(1).astype(jnp.int32)
    swap = [(0, 1), (1, 0)]
    height, width = counts.shape
    rank = sketch.shape[1]
    half = width // 2

    row_local = copy_for_each(row_support, "col").reshape(-1)
    col_local = copy_for_each(col_support, ROW).reshape(-1)
    table, part = lift(counts, row_local, col_local, total, sketch)

    arrived = exchange(part.reshape(cols, -1, rank), "col")
    first = exchange(sum_and_spread(arrived, cols), "col").reshape(height, rank)
    grams = exchange(call(first_gram_body, shaped((rows, LEAD, rank)), first), ROW)
    cleared, sent = call(
        send_half_body,
        (shaped((height, rank), BF16), shaped((half, rank))),
        core,
        grams,
        first,
        table,
        in_specs=[SM, VM, VM, VM],
        vmem=40,
    )
    got = lax.ppermute(sent, "core", swap)
    kept = call(keep_half_body, shaped((half, rank)), core, cleared, table, in_specs=[SM, VM, VM], vmem=40)
    both = call(add_body, shaped((half, rank), BF16), kept, got)

    parts = exchange(both.reshape(planes, -1, rank), PLANE)
    piece, grams = call(
        second_gram_body, (shaped(parts.shape[1:]), shaped((rows, LEAD, rank))), parts
    )
    grams = exchange(sum_and_spread(exchange(grams, ROW), cols), "col")
    mine = call(clear_body, shaped(parts.shape, BF16), grams, piece)
    mine = exchange(mine, PLANE).reshape(half, rank)
    other = lax.ppermute(mine, "core", swap)

    packed = call(
        third_body,
        shaped((cols, height // cols + rank // cols, rank)),
        core,
        mine,
        other,
        table,
        in_specs=[SM, VM, VM, VM],
        vmem=40,
    )
    packed = exchange(sum_and_spread(exchange(packed, "col"), cols), "col")
    value = packed[:, : height // cols].reshape(height, rank)
    second = packed[:, height // cols :].reshape(rank, rank)
    gram = call(third_gram_body, shaped((rank, rank)), value)
    gram = exchange(sum_and_spread(exchange(gram.reshape(rows, -1, rank), ROW), rows), ROW)
    return tuple(
        call(
            functools.partial(last_body, float(height * rows) ** 0.5, float(width * cols) ** 0.5),
            (shaped((height, rank)), shaped((width, rank))),
            core,
            second,
            gram.reshape(rank, rank),
            mine,
            other,
            value,
            in_specs=[SM, VM, VM, VM, VM, VM],
            scratch_shapes=[pltpu.VMEM((rank, rank), F32), pltpu.VMEM((rank, rank), F32)],
            vmem=40,
        )
    )


def solution(mesh):
    grid = Mesh(mesh.devices.reshape(8, 2, 2, mesh.shape["col"]), ("z", "far", "core", "col"))
    in_specs = (P(ROW, "col"), P((*ROW, "col")), P(("col", *ROW)), P(), P("col", None))
    out_specs = (P(ROW, None), P("col", None))
    return jax.shard_map(per_device, mesh=grid, in_specs=in_specs, out_specs=out_specs, check_vma=False)
```

time: 600 us -> 301 us (0.50)
  other arithmetic: 182 us -> 0.66 us
  waiting for transfers between devices: 93.8 us -> 41.6 us
  Pallas kernels: 0 us -> 38.4 us
  blocking collectives: 214 us -> 176 us
  local copies, waits for them, and re-layouts: 43.1 us -> 13.7 us
  matrix products: 18.6 us -> 0 us
  starting transfers between devices: 36.3 us -> 28.7 us
    another operation x27 -> x0, other arithmetic: 163 us -> none  [the longest x20 103 us: factor_of(): return jnp.linalg.cholesky(gram)]
    all_to_all x6 -> x3, waiting for transfers between devices: 93.8 us -> 36.3 us  [exchange(): return lax.all_to_all(parts, axes, 0, 0, tiled=True)]
    pallas_call x0 -> x14, Pallas kernels: none -> 38.4 us  [call(): pl.pallas_call(body, out_shape=out_shape, compiler_params=pltpu.CompilerP...]
    all_to_all x7 -> x10, blocking collectives: 214 us -> 176 us  [exchange(): return lax.all_to_all(parts, axes, 0, 0, tiled=True)]
    another operation x30 -> x1, local copies, waits for them, and re-layouts: 17.9 us -> 0.2 us  [lift(): rows.reshape(height, 1)]
    all_to_all x6 -> x3, starting transfers between devices: 36.3 us -> 23.6 us  [exchange(): return lax.all_to_all(parts, axes, 0, 0, tiled=True)]
    another operation x15 -> x0, matrix products: 11.3 us -> none  [the longest x9 9.92 us: solve_rows(): return jax.scipy.linalg.solve_triangular(lower, matrix.T, lower=True).T]
    reduce_sum x7 -> x0, other arithmetic: 9.71 us -> none  [the longest x3 5.18 us: taken_together(): return copy_for_each(shard, axis).sum(axis=0)]
  transfers between devices with their start and end apart: 6 -> 5, of which waited for: 6 -> 5; matrix products, arithmetic and copies ran while one was open for 3% -> 1% of each run, Pallas kernels for 0% -> 0%
where the time goes in v1:
time: 301 us; the launch traced here: 300 us
  blocking collectives  176 us (58%)
  waiting for transfers between devices  41.6 us (14%)
  Pallas kernels  38.4 us (13%)
  starting transfers between devices  28.7 us (10%)
  local copies, waits for them, and re-layouts  13.7 us (5%)
    all_to_all x10, blocking collectives, exchange(): return lax.all_to_all(parts, axes, 0, 0, tiled=True)  176 us
    pallas_call x14, Pallas kernels, call(): pl.pallas_call(body, out_shape=out_shape, compiler_params=pltpu.CompilerP...  38.4 us
    all_to_all x3, waiting for transfers between devices, exchange(): return lax.all_to_all(parts, axes, 0, 0, tiled=True)  36.3 us
    all_to_all x3, starting transfers between devices, exchange(): return lax.all_to_all(parts, axes, 0, 0, tiled=True)  23.6 us
    unnamed x10, local copies, waits for them, and re-layouts  10 us
  transfers between devices with their start and end apart: 5, of which 5 were waited for; matrix products, arithmetic and copies ran while one was open for 1% of the time, Pallas kernels for 0%

profile of v1, /device:TPU:1, one launch (start us, length us, event | category | flops | bytes accessed | tf_op | source)
XLA Modules:
  0.0 300.3 jit_solution(15742276095686567463)
XLA Ops:
  1.3 10.8 %all_to_all.67 = s32[8,1,64]{2,1,0:T(1,128)S(1)} all-to-all(s32[8,1,64]{2,1,0:T(1,128)S(1)} %broadcast_in_dim.4), channel_id=1, replica_groups=mesh['z'=8,'far'=2,'core'=2,'col'=8] {'col'}, dimensions={0} | all-to-all | bytes 4096 | tf_op jit(solution)/shard_map/all_to_all | solution.py:34
  12.0 1.3 broadcast_in_dim.5
  13.3 12.9 %all-to-all-start.1 = ((s32[32,1,128]{2,1,0:T(1,128)}), s32[32,1,128]{2,1,0:T(1,128)S(1)}, u32[]{:S(2)}, u32[]{:S(2)}) async-start(s32[32,1,128]{2,1,0:T(1,128)} %broadcast_in_dim.5), calls=%async_computation.1 | async-start | bytes 32768 | tf_op jit(solution)/shard_map/all_to_all | solution.py:34
  28.2 7.3 %all-to-all-done.1 = s32[32,1,128]{2,1,0:T(1,128)S(1)} async-done(((s32[32,1,128]{2,1,0:T(1,128)}), s32[32,1,128]{2,1,0:T(1,128)S(1)}, u32[]{:S(2)}, u32[]{:S(2)}) %all-to-all-start.1) | async-done | bytes 16416 | tf_op jit(solution)/shard_map/all_to_all | solution.py:34
  35.5 3.4 %copy-done.2 = s32[512,4096]{1,0:T(8,128)S(1)} copy-done((s32[512,4096]{1,0:T(8,128)S(1)}, s32[512,4096]{1,0:T(8,128)}, u32[]{:S(2)}) %copy-start.2) | copy-done | bytes 8388632
  38.9 1.6 copy-done.3
  40.5 5.8 %shard_map.68 = (bf16[512,4096]{1,0:T(8,128)(2,1)S(1)}, f32[512,256]{1,0:T(8,128)S(1)}) custom-call(s32[512,4096]{1,0:T(8,128)S(1)} %copy-done.2, s32[512,1]{1,0:T(8,128)S(1)} %reshape_reshape.8.rows, s32[1,4096]{1,0:T(1,128)S(1)} %bitcast.24, s32[1,1]{1,0:T(1,128)} %bitcast.11.total, bf16[4096,256]{1,0:T(8,128)(2,1)S(1)} %copy-done.3), custom_call_target="tpu_custom_call" | custom-call | tf_op jit(solution)/shard_map/pallas_call | solution.py:21
  46.3 2.0 copy-done
  48.3 11.2 %all_to_all.68.parts = f32[8,64,256]{2,1,0:T(8,128)S(1)} all-to-all(f32[8,64,256]{2,1,0:T(8,128)S(1)} %bitcast.23), channel_id=1, replica_groups=mesh['z'=8,'far'=2,'core'=2,'col'=8] {'col'}, dimensions={0} | all-to-all | bytes 1048576 | tf_op jit(solution)/shard_map/all_to_all | solution.py:34
  59.6 11.6 %all_to_all.69 = f32[8,64,256]{2,1,0:T(8,128)S(1)} all-to-all(f32[8,64,256]{2,1,0:T(8,128)S(1)} %shard_map.69), channel_id=1, replica_groups=mesh['z'=8,'far'=2,'core'=2,'col'=8] {'col'}, dimensions={0} | all-to-all | bytes 1048576 | tf_op jit(solution)/shard_map/all_to_all | solution.py:34
  71.2 1.3 shard_map.70
  72.5 6.3 %all-to-all-start.4 = ((f32[32,16,256]{2,1,0:T(8,128)}), f32[32,16,256]{2,1,0:T(8,128)S(1)}, u32[]{:S(2)}, u32[]{:S(2)}) async-start(f32[32,16,256]{2,1,0:T(8,128)} %shard_map.70), calls=%async_computation.4 | async-start | bytes 1048576 | tf_op jit(solution)/shard_map/all_to_all | solution.py:34
  78.8 17.3 %all-to-all-done.4.grams = f32[32,16,256]{2,1,0:T(8,128)S(1)} async-done(((f32[32,16,256]{2,1,0:T(8,128)}), f32[32,16,256]{2,1,0:T(8,128)S(1)}, u32[]{:S(2)}, u32[]{:S(2)}) %all-to-all-start.4) | async-done | bytes 524320 | tf_op jit(solution)/shard_map/all_to_all | solution.py:34
  96.1 2.2 copy-done.1
  98.3 2.5 shard_map.71
  100.8 1.1 collective-permute-start
  102.8 3.0 collective-permute-done.right
  105.9 32.6 %all_to_all.70.parts = bf16[16,128,256]{2,1,0:T(8,128)(2,1)S(1)} all-to-all(bf16[16,128,256]{2,1,0:T(8,128)(2,1)S(1)} %bitcast.19), channel_id=1, replica_groups=mesh['z'=8,'far'=2,'core'=2,'col'=8] {'z','far'}, dimensions={0} | all-to-all | bytes 2097152 | tf_op jit(solution)/shard_map/all_to_all | solution.py:34
  139.0 22.6 %all_to_all.71.parts = f32[32,16,256]{2,1,0:T(8,128)S(1)} all-to-all(f32[32,16,256]{2,1,0:T(8,128)S(1)} %get-tuple-element.12), channel_id=1, replica_groups=mesh['z'=8,'far'=2,'core'=2,'col'=8] {'z','far','core'}, dimensions={0} | all-to-all | bytes 1048576 | tf_op jit(solution)/shard_map/all_to_all | solution.py:34
  161.6 7.8 %all_to_all.72.grams = f32[8,16,256]{2,1,0:T(8,128)S(1)} all-to-all(f32[8,16,256]{2,1,0:T(8,128)S(1)} %shard_map.75), channel_id=1, replica_groups=mesh['z'=8,'far'=2,'core'=2,'col'=8] {'col'}, dimensions={0} | all-to-all | bytes 262144 | tf_op jit(solution)/shard_map/all_to_all | solution.py:34
  169.5 0.9 shard_map.76
  170.4 31.8 %all_to_all.73 = bf16[16,128,256]{2,1,0:T(8,128)(2,1)S(1)} all-to-all(bf16[16,128,256]{2,1,0:T(8,128)(2,1)S(1)} %shard_map.76), channel_id=1, replica_groups=mesh['z'=8,'far'=2,'core'=2,'col'=8] {'z','far'}, dimensions={0} | all-to-all | bytes 2097152 | tf_op jit(solution)/shard_map/all_to_all | solution.py:34
  202.2 4.0 %collective-permute-start.1 = (bf16[2048,256]{1,0:T(8,128)(2,1)S(1)}, bf16[2048,256]{1,0:T(8,128)(2,1)S(1)}, u32[]{:S(2)}, u32[]{:S(2)}) collective-permute-start(bf16[2048,256]{1,0:T(8,128)(2,1)S(1)} %bitcast.12), channel_id=1, source_target_pairs={{0,8},{8,0},{1,9},{9,1},{2,10},{10,2},{3,11},{11,3},{4,12},{12,4},... | collective-permute-start | bytes 3145736 | tf_op jit(solution)/shard_map/ppermute | solution.py:314
  206.2 2.3 collective-permute-done.1.other
  208.5 1.8 shard_map.77
  210.3 14.0 %all_to_all.74.parts = f32[8,96,256]{2,1,0:T(8,128)S(1)} all-to-all(f32[8,96,256]{2,1,0:T(8,128)S(1)} %shard_map.77), channel_id=1, replica_groups=mesh['z'=8,'far'=2,'core'=2,'col'=8] {'col'}, dimensions={0} | all-to-all | bytes 1572864 | tf_op jit(solution)/shard_map/all_to_all | solution.py:34
  224.4 15.5 %all_to_all.75 = f32[8,96,256]{2,1,0:T(8,128)S(1)} all-to-all(f32[8,96,256]{2,1,0:T(8,128)S(1)} %shard_map.78), channel_id=1, replica_groups=mesh['z'=8,'far'=2,'core'=2,'col'=8] {'col'}, dimensions={0} | all-to-all | bytes 1572864 | tf_op jit(solution)/shard_map/all_to_all | solution.py:34
  241.5 18.0 %all_to_all.76.parts = f32[32,8,256]{2,1,0:T(8,128)S(1)} all-to-all(f32[32,8,256]{2,1,0:T(8,128)S(1)} %bitcast.20), channel_id=1, replica_groups=mesh['z'=8,'far'=2,'core'=2,'col'=8] {'z','far','core'}, dimensions={0} | all-to-all | bytes 524288 | tf_op jit(solution)/shard_map/all_to_all | solution.py:34
  260.2 4.3 %all-to-all-start.12 = ((f32[32,8,256]{2,1,0:T(8,128)}), f32[32,8,256]{2,1,0:T(8,128)S(1)}, u32[]{:S(2)}, u32[]{:S(2)}) async-start(f32[32,8,256]{2,1,0:T(8,128)} %shard_map.80), calls=%async_computation.12 | async-start | bytes 524288 | tf_op jit(solution)/shard_map/all_to_all | solution.py:34
  264.5 1.0 slice.8
  265.5 11.8 %all-to-all-done.12 = f32[32,8,256]{2,1,0:T(8,128)S(1)} async-done(((f32[32,8,256]{2,1,0:T(8,128)}), f32[32,8,256]{2,1,0:T(8,128)S(1)}, u32[]{:S(2)}, u32[]{:S(2)}) %all-to-all-start.12) | async-done | bytes 262176 | tf_op jit(solution)/shard_map/all_to_all | solution.py:34
  277.3 23.0 %shard_map.81 = (f32[512,256]{1,0:T(8,128)}, f32[4096,256]{1,0:T(8,128)}) custom-call(s32[1]{0:T(128)} %bitcast.core, f32[256,256]{1,0:T(8,128)S(1)} %bitcast.22, f32[256,256]{1,0:T(8,128)S(1)} %bitcast.21, bf16[2048,256]{1,0:T(8,128)(2,1)S(1)} %bitcast.14, bf16[2048,256]{1,0:T(8,128)(2,1)S(1)} %collective-permute-done.1.other, f32[512,256]{1,0:T(8,128)S(1)} %bitcast.16), custom_call_target="tpu_custom_call" | custom-call | tf_op jit(solution)/shard_map/pallas_call | solution.py:21
  (19 shorter events, 6.0 us)
Async XLA Ops:
  13.3 22.2 %all-to-all-start.1 = ((s32[32,1,128]{2,1,0:T(1,128)}), s32[32,1,128]{2,1,0:T(1,128)S(1)}, u32[]{:S(2)}, u32[]{:S(2)}) async-start(s32[32,1,128]{2,1,0:T(1,128)} %broadcast_in_dim.5), calls=%async_computation.1 | async-start | bytes 32768 | tf_op jit(solution)/shard_map/all_to_all | solution.py:34
  35.5 3.4 %copy-start.2 = (s32[512,4096]{1,0:T(8,128)S(1)}, s32[512,4096]{1,0:T(8,128)}, u32[]{:S(2)}) copy-start(s32[512,4096]{1,0:T(8,128)} %counts.1) | copy-start | bytes 25165828
  38.9 1.6 copy-start.3
  46.3 2.0 copy-start
  72.5 23.7 %all-to-all-start.4 = ((f32[32,16,256]{2,1,0:T(8,128)}), f32[32,16,256]{2,1,0:T(8,128)S(1)}, u32[]{:S(2)}, u32[]{:S(2)}) async-start(f32[32,16,256]{2,1,0:T(8,128)} %shard_map.70), calls=%async_computation.4 | async-start | bytes 1048576 | tf_op jit(solution)/shard_map/all_to_all | solution.py:34
  96.1 2.2 copy-start.1
  100.8 4.9 %collective-permute-start = (f32[2048,256]{1,0:T(8,128)S(1)}, f32[2048,256]{1,0:T(8,128)S(1)}, u32[]{:S(2)}, u32[]{:S(2)}) collective-permute-start(f32[2048,256]{1,0:T(8,128)S(1)} %get-tuple-element.11), channel_id=1, source_target_pairs={{0,8},{8,0},{1,9},{9,1},{2,10},{10,2},{3,11},{11,3},{4,12},{12,4},... | collective-permute-start | bytes 6291464 | tf_op jit(solution)/shard_map/ppermute | solution.py:303
  202.2 6.3 %collective-permute-start.1 = (bf16[2048,256]{1,0:T(8,128)(2,1)S(1)}, bf16[2048,256]{1,0:T(8,128)(2,1)S(1)}, u32[]{:S(2)}, u32[]{:S(2)}) collective-permute-start(bf16[2048,256]{1,0:T(8,128)(2,1)S(1)} %bitcast.12), channel_id=1, source_target_pairs={{0,8},{8,0},{1,9},{9,1},{2,10},{10,2},{3,11},{11,3},{4,12},{12,4},... | collective-permute-start | bytes 3145736 | tf_op jit(solution)/shard_map/ppermute | solution.py:314
  239.9 0.9 copy-start.4
  260.2 17.1 %all-to-all-start.12 = ((f32[32,8,256]{2,1,0:T(8,128)}), f32[32,8,256]{2,1,0:T(8,128)S(1)}, u32[]{:S(2)}, u32[]{:S(2)}) async-start(f32[32,8,256]{2,1,0:T(8,128)} %shard_map.80), calls=%async_computation.12 | async-start | bytes 524288 | tf_op jit(solution)/shard_map/all_to_all | solution.py:34

commit v2 on v1

v2 whole, which is shorter than its diff:
```python
import functools

import jax
import jax.numpy as jnp
from jax import lax
from jax.experimental import pallas as pl
from jax.experimental.pallas import tpu as pltpu
from jax.sharding import Mesh
from jax.sharding import PartitionSpec as P

PLANE = ("z", "far")
ROW = ("z", "far", "core")
F32 = jnp.float32
BF16 = jnp.bfloat16
EXACT = lax.Precision.HIGHEST
LEAD = 16
FEW = 8
ABSENT = -1e30
RIDGE = 1e-6
TINY = 1e-20
BLOCK = 32


def call(body, out_shape, *args, **options):
    return pl.pallas_call(
        body,
        out_shape=out_shape,
        compiler_params=pltpu.CompilerParams(vmem_limit_bytes=options.pop("vmem", 12) << 20),
        **options,
    )(*args)


def shaped(shape, dtype=F32):
    return jax.ShapeDtypeStruct(shape, dtype)


def in_hbm(value):
    return pltpu.with_memory_space_constraint(value, pltpu.HBM)


def exchange(parts, axes):
    return lax.all_to_all(parts, axes, 0, 0, tiled=True)


def copy_for_each(shard, axes):
    count = lax.axis_size(axes)
    return exchange(jnp.broadcast_to(shard[None], (count, *shard.shape)), axes)


def over_rows(left, right, precision=None):
    return lax.dot_general(
        left, right, (((0,), (0,)), ((), ())), precision=precision, preferred_element_type=F32
    )


def over_lanes(left, right, precision=None):
    return lax.dot_general(
        left, right, (((1,), (1,)), ((), ())), precision=precision, preferred_element_type=F32
    )


def log_body(counts, total, out):
    block = counts[...]
    value = jnp.log(jnp.maximum(block, 1).astype(F32)) + jnp.log(total[...].astype(F32))
    out[...] = jnp.where(block > 0, value, ABSENT)


def logs_of(counts, total, wide=512):
    height, width = counts.shape
    return call(
        log_body,
        pltpu.HBM((height, width), F32),
        in_hbm(counts),
        total.reshape(1, 1),
        grid=(width // wide,),
        in_specs=[pl.BlockSpec((height, wide), lambda i: (0, i)), pl.BlockSpec((1, 1), lambda i: (0, 0))],
        out_specs=pl.BlockSpec((height, wide), lambda i: (0, i)),
        vmem=12,
    )


def lift_body(logs, rows, cols, sketch, table, part, acc):
    step = pl.program_id(0)
    value = logs[...] - jnp.log(rows[...].astype(F32)) - jnp.log(cols[...].astype(F32))
    lifted = jnp.maximum(value, 0.0).astype(BF16)
    table[...] = lifted
    added = jnp.dot(lifted, sketch[...], preferred_element_type=F32)

    @pl.when(step == 0)
    def _():
        acc[...] = added

    @pl.when(step > 0)
    def _():
        acc[...] += added

    @pl.when(step == pl.num_programs(0) - 1)
    def _():
        part[...] = acc[...]


def lift(logs, rows, cols, sketch, wide=512):
    height, width = logs.shape
    rank = sketch.shape[1]
    return call(
        lift_body,
        (pltpu.HBM((height, width), BF16), shaped((height, rank))),
        in_hbm(logs),
        rows.reshape(height, 1),
        cols.reshape(1, width),
        sketch,
        grid=(width // wide,),
        in_specs=[
            pl.BlockSpec((height, wide), lambda i: (0, i)),
            pl.BlockSpec((height, 1), lambda i: (0, 0)),
            pl.BlockSpec((1, wide), lambda i: (0, i)),
            pl.BlockSpec((wide, rank), lambda i: (i, 0)),
        ],
        out_specs=[
            pl.BlockSpec((height, wide), lambda i: (0, i)),
            pl.BlockSpec((height, rank), lambda i: (0, 0)),
        ],
        scratch_shapes=[pltpu.VMEM((height, rank), F32)],
        vmem=12,
    )


def summed(ref):
    value = ref[0].astype(F32)
    for i in range(1, ref.shape[0]):
        value = value + ref[i].astype(F32)
    return value


def spread_body(parts, out):
    value = summed(parts)
    for i in range(out.shape[0]):
        out[i] = value


def sum_and_spread(parts, count):
    return call(spread_body, shaped((count, *parts.shape[1:])), parts)


def diag_inverse(tile, lane0, size):
    groups = size // 8
    sub = lax.broadcasted_iota(jnp.int32, (8, 128), 0)
    lane = lax.broadcasted_iota(jnp.int32, (8, 128), 1)
    col = [
        {
            g: jnp.broadcast_to(tile[8 * g : 8 * g + 8, lane0 + j : lane0 + j + 1], (8, 128))
            for g in range(j // 8, groups)
        }
        for j in range(size)
    ]
    inv = [jnp.where(lane == sub + (lane0 + 8 * g), 1.0, 0.0).astype(F32) for g in range(groups)]
    scale = [jnp.zeros((8, 128), F32) for _ in range(groups)]

    def row(value, i):
        return jnp.broadcast_to(value[i : i + 1, :], (8, 128))

    for j in range(size):
        gj, sj = divmod(j, 8)
        root = lax.rsqrt(row(col[j][gj], sj))
        scale[gj] = jnp.where(sub == sj, root, scale[gj])
        over = root * root
        part = {g: col[j][g] * over for g in range(gj, groups)}
        part[gj] = jnp.where(sub > sj, part[gj], 0.0)
        for k in range(j + 1, size):
            pivot = row(col[j][k // 8], k % 8)
            for g in range(k // 8, groups):
                col[k][g] = col[k][g] - part[g] * pivot
        own = row(inv[gj], sj)
        for g in range(gj, groups):
            inv[g] = inv[g] - part[g] * own
    return jnp.concatenate([inv[g] * scale[g] for g in range(groups)], axis=0)


def invert_factor(m, size=BLOCK):
    n = m.shape[0]
    for r0 in range(0, n, size):
        t0 = r0 // 128 * 128
        inv = diag_inverse(m[r0 : r0 + size, t0 : t0 + 128], r0 - t0, size)
        rows = jnp.dot(inv, m[t0 : t0 + 128, :], precision=EXACT, preferred_element_type=F32)
        column = lax.broadcasted_iota(jnp.int32, (size, n), 1)
        wide = jnp.concatenate([inv if t == t0 else jnp.zeros_like(inv) for t in range(0, n, 128)], axis=1)
        done = jnp.where((column >= r0) & (column < r0 + size), wide, rows)
        m[r0 : r0 + size, :] = done
        if r0 + size < n:
            base = (r0 + size) // 128 * 128
            left = jnp.where(column >= r0 + size, rows, 0.0)[:, base:]
            change = over_rows(left, done, EXACT)
            below = m[r0 + size :, :]
            at = lax.broadcasted_iota(jnp.int32, below.shape, 1)
            below = jnp.where((at >= r0) & (at < r0 + size), 0.0, below)
            m[r0 + size :, :] = below - change[r0 + size - base :, :]
    i = lax.broadcasted_iota(jnp.int32, (n, n), 0)
    j = lax.broadcasted_iota(jnp.int32, (n, n), 1)
    return jnp.where(i >= j, m[...], 0.0)


def lead_rows(gram):
    lead, rank = gram.shape
    i = lax.broadcasted_iota(jnp.int32, (lead, rank), 0)
    j = lax.broadcasted_iota(jnp.int32, (lead, rank), 1)
    size = jnp.sum(jnp.sum(jnp.where(i == j, gram, 0.0), axis=1, keepdims=True), axis=0, keepdims=True)
    gram = gram + jnp.where(i == j, size * RIDGE + TINY, 0.0)
    inv = diag_inverse(gram[:, :128], 0, lead)[:, :lead]
    solved = over_rows(inv, jnp.dot(inv, gram, precision=EXACT, preferred_element_type=F32), EXACT)
    return inv, solved, jnp.where(i == j, 1.0, 0.0), j < lead, size


def lead_change(gram):
    inv, solved, unit, lead, size = lead_rows(gram)
    own = over_rows(inv, unit, EXACT) * jnp.sqrt(size / gram.shape[0]) - unit
    return jnp.where(lead, own, -solved)


def lead_out(value, change):
    lead = change.shape[0]
    return value + jnp.dot(value[:, :lead], change, precision=EXACT, preferred_element_type=F32)


def split(value):
    high = value.astype(BF16)
    return high, (value - high.astype(F32)).astype(BF16)


def half_body(core, value, table, out, high, low):
    del core

    @pl.when(pl.program_id(0) == 0)
    def _():
        high[...], low[...] = split(value[...])

    columns = table[...]
    out[...] = over_rows(columns, high[...]) + over_rows(columns, low[...])


def half_product(other, core, value, table, wide=512):
    height, rank = value.shape
    half = table.shape[1] // 2
    steps = half // wide

    def at(i, core):
        return (0, (1 - core[0] if other else core[0]) * steps + i)

    return call(
        half_body,
        shaped((half, rank)),
        core,
        value,
        in_hbm(table),
        grid_spec=pltpu.PrefetchScalarGridSpec(
            num_scalar_prefetch=1,
            grid=(steps,),
            in_specs=[
                pl.BlockSpec((height, rank), lambda i, core: (0, 0)),
                pl.BlockSpec((height, wide), at),
            ],
            out_specs=pl.BlockSpec((wide, rank), lambda i, core: (i, 0)),
            scratch_shapes=[pltpu.VMEM((height, rank), BF16), pltpu.VMEM((height, rank), BF16)],
        ),
    )


def encode(value, out, count):
    tall, rank = value.shape
    deep = tall // count
    inv, solved, unit, lead, size = lead_rows(over_rows(value[:, :128], value, EXACT)[:FEW, :])
    across = jnp.where(lead, unit, solved).astype(BF16).astype(F32)
    lane = lax.broadcasted_iota(jnp.int32, (tall, 128), 1)
    down = jnp.where(lane < FEW, value[:, :128], 0.0).astype(BF16)
    turned = over_lanes(unit[:, :128].astype(BF16), down)
    rest = (value - over_rows(turned, across)).astype(BF16)
    for k in range(out.shape[0]):
        own = k % count * deep
        out[k, :deep, :] = rest[own : own + deep, :]
        tail = jnp.concatenate([turned[:, own : own + deep], jnp.zeros((FEW, rank - deep), F32)], axis=1)
        out[k, deep:, :] = jnp.concatenate([across, tail], axis=0).astype(BF16)


def encode_sum_body(left, right, out):
    encode(left[...] + right[...], out, out.shape[0])


def encode_parts_body(parts, out):
    count, tall, rank = parts.shape
    deep = tall - 2 * FEW
    tails = [parts[k, deep:, :].astype(F32) for k in range(count)]
    down = jnp.concatenate([tail[FEW:, :deep] for tail in tails], axis=0)
    across = jnp.concatenate([tail[:FEW, :] for tail in tails], axis=0)
    value = over_rows(down, across)
    for k in range(count):
        value = value + parts[k, :deep, :].astype(F32)
    encode(value, out, 1)


def decode_body(core, mine, other, value, out):
    count, tall, rank = mine.shape
    deep = tall - 2 * FEW
    for source, at in ((mine, core[0]), (other, 1 - core[0])):
        for k in range(count):
            tail = source[k, deep:, :].astype(F32)
            block = source[k, :deep, :].astype(F32) + over_rows(tail[FEW:, :deep], tail[:FEW, :])
            start = pl.multiple_of(at * (count * deep) + k * deep, deep)
            value[pl.ds(start, deep), :] = block
    total = jnp.zeros((128, rank), F32)
    for start in range(0, value.shape[0], 512):
        block = value[start : start + 512, :]
        total = total + over_rows(block[:, :128], block, EXACT)
    for i in range(out.shape[0]):
        out[i] = total[:LEAD, :]


def third_body(grams, value, table, second, out):
    cleared = lead_out(value[...], lead_change(summed(grams))).astype(BF16)
    second[...] = cleared
    product = jnp.dot(table[...], cleared, preferred_element_type=F32)
    gram = over_rows(cleared, cleared)
    count = out.shape[0]
    deep, thin = product.shape[0] // count, gram.shape[0] // count
    for i in range(count):
        out[i, :deep, :] = product[i * deep : (i + 1) * deep, :]
        out[i, deep:, :] = gram[i * thin : (i + 1) * thin, :]


def unpacked(packed, start, stop):
    return jnp.concatenate([packed[i, start:stop, :] for i in range(packed.shape[0])], axis=0)


def third_gram_body(packed, out):
    value = unpacked(packed, 0, packed.shape[1] - packed.shape[2] // packed.shape[0])
    gram = over_rows(value, value, EXACT)
    thin = out.shape[1]
    for i in range(out.shape[0]):
        out[i] = gram[i * thin : (i + 1) * thin, :]


def right_body(root, packed, second, out, work):
    work[...] = unpacked(packed, packed.shape[1] - packed.shape[2] // packed.shape[0], packed.shape[1])
    high, low = split(invert_factor(work) * root)
    deep = second.shape[0] // 8
    for i in range(8):
        part = second[i * deep : (i + 1) * deep, :]
        out[i * deep : (i + 1) * deep, :] = over_lanes(part, high) + over_lanes(part, low)


def left_body(root, packed, third, out, work):
    work[...] = third[...]
    value = unpacked(packed, 0, packed.shape[1] - packed.shape[2] // packed.shape[0])
    out[...] = over_lanes(value, invert_factor(work) * root, EXACT)


VM = pl.BlockSpec(memory_space=pltpu.VMEM)
SM = pl.BlockSpec(memory_space=pltpu.SMEM)


def per_device(counts, row_support, col_support, total, sketch):
    rows, cols, planes = lax.axis_size(ROW), lax.axis_size("col"), lax.axis_size(PLANE)
    core = lax.axis_index("core").reshape(1).astype(jnp.int32)
    swap = [(0, 1), (1, 0)]
    height, width = counts.shape
    rank = sketch.shape[1]
    half = width // 2

    row_local = copy_for_each(row_support, "col").reshape(-1)
    col_local = copy_for_each(col_support, ROW).reshape(-1)
    logs = logs_of(counts, total)
    table, part = lift(logs, row_local, col_local, sketch)

    arrived = exchange(part.reshape(cols, -1, rank), "col")
    first = exchange(sum_and_spread(arrived, cols), "col").reshape(height, rank)
    sides = [half_product(other, core, first, table) for other in (True, False)]
    got = lax.ppermute(sides[0], "core", swap)
    deep = half // planes
    coded = shaped((planes, deep + 2 * FEW, rank), BF16)
    parts = exchange(call(encode_sum_body, coded, sides[1], got, vmem=16), PLANE)
    mine = call(encode_parts_body, coded, parts, vmem=12)
    mine = exchange(mine, PLANE)
    other = lax.ppermute(mine, "core", swap)
    value, grams = call(
        decode_body,
        (shaped((width, rank)), shaped((cols, LEAD, rank))),
        core,
        mine,
        other,
        in_specs=[SM, VM, VM],
        vmem=20,
    )
    grams = exchange(grams, "col")
    second, packed = call(
        third_body,
        (shaped((width, rank), BF16), shaped((cols, height // cols + rank // cols, rank))),
        grams,
        value,
        table,
        vmem=24,
    )
    packed = exchange(sum_and_spread(exchange(packed, "col"), cols), "col")
    gram = call(third_gram_body, shaped((rows, rank // rows, rank)), packed, vmem=12)
    gram = exchange(sum_and_spread(exchange(gram, ROW), rows), ROW)
    work = [pltpu.VMEM((rank, rank), F32)]
    right = call(
        functools.partial(right_body, float(width * cols) ** 0.5),
        shaped((width, rank)),
        packed,
        second,
        scratch_shapes=work,
        vmem=20,
    )
    left = call(
        functools.partial(left_body, float(height * rows) ** 0.5),
        shaped((height, rank)),
        packed,
        gram.reshape(rank, rank),
        scratch_shapes=work,
        vmem=12,
    )
    return left, right


def solution(mesh):
    grid = Mesh(mesh.devices.reshape(8, 2, 2, mesh.shape["col"]), ("z", "far", "core", "col"))
    in_specs = (P(ROW, "col"), P((*ROW, "col")), P(("col", *ROW)), P(), P("col", None))
    out_specs = (P(ROW, None), P("col", None))
    return jax.shard_map(per_device, mesh=grid, in_specs=in_specs, out_specs=out_specs, check_vma=False)
```

time: 301 us -> 266 us (0.88)
  Pallas kernels: 38.4 us -> 70.4 us
  waiting for transfers between devices: 41.6 us -> 10.2 us
  blocking collectives: 176 us -> 153 us
  local copies, waits for them, and re-layouts: 13.7 us -> 2.65 us
    pallas_call x14, Pallas kernels: 38.4 us -> 70.4 us  [call(): pl.pallas_call(body, out_shape=out_shape, compiler_params=pltpu.CompilerP...]
    all_to_all x3, waiting for transfers between devices: 36.3 us -> 7.63 us  [exchange(): return lax.all_to_all(parts, axes, 0, 0, tiled=True)]
    all_to_all x10 -> x8, blocking collectives: 176 us -> 153 us  [exchange(): return lax.all_to_all(parts, axes, 0, 0, tiled=True)]
    unnamed x10 -> x4, local copies, waits for them, and re-layouts: 10 us -> 0.01 us
  transfers between devices with their start and end apart: 5 -> 5, of which waited for: 5 -> 3; matrix products, arithmetic and copies ran while one was open for 1% -> 1% of each run, Pallas kernels for 0% -> 10%
where the time goes in v2:
time: 266 us; the launch traced here: 265 us
  blocking collectives  153 us (58%)
  Pallas kernels  70.4 us (26%)
  starting transfers between devices  26.6 us (10%)
  waiting for transfers between devices  10.2 us (4%)
    all_to_all x8, blocking collectives, exchange(): return lax.all_to_all(parts, axes, 0, 0, tiled=True)  153 us
    pallas_call x14, Pallas kernels, call(): pl.pallas_call(body, out_shape=out_shape, compiler_params=pltpu.CompilerP...  70.4 us
    all_to_all x3, starting transfers between devices, exchange(): return lax.all_to_all(parts, axes, 0, 0, tiled=True)  21.4 us
    all_to_all x3, waiting for transfers between devices, exchange(): return lax.all_to_all(parts, axes, 0, 0, tiled=True)  7.63 us
  transfers between devices with their start and end apart: 5, of which 3 were waited for; matrix products, arithmetic and copies ran while one was open for 1% of the time, Pallas kernels for 10%

profile of v2, /device:TPU:1, one launch (start us, length us, event | category | flops | bytes accessed | tf_op | source)
XLA Modules:
  0.0 265.1 jit_solution(16550703404537235093)
XLA Ops:
  0.6 0.7 broadcast_in_dim.4
  1.3 10.8 %all_to_all.57 = s32[8,1,64]{2,1,0:T(1,128)S(1)} all-to-all(s32[8,1,64]{2,1,0:T(1,128)S(1)} %broadcast_in_dim.4), channel_id=1, replica_groups=mesh['z'=8,'far'=2,'core'=2,'col'=8] {'col'}, dimensions={0} | all-to-all | bytes 4096 | tf_op jit(solution)/shard_map/all_to_all | solution.py:42
  12.0 1.3 broadcast_in_dim.5
  13.3 12.9 %all-to-all-start.1 = ((s32[32,1,128]{2,1,0:T(1,128)}), s32[32,1,128]{2,1,0:T(1,128)S(1)}, u32[]{:S(2)}, u32[]{:S(2)}) async-start(s32[32,1,128]{2,1,0:T(1,128)} %broadcast_in_dim.5), calls=%async_computation.1 | async-start | bytes 32768 | tf_op jit(solution)/shard_map/all_to_all | solution.py:42
  26.9 10.4 %shard_map.68.logs = f32[512,4096]{1,0:T(8,128)} custom-call(s32[512,4096]{1,0:T(8,128)} %counts.1, s32[1,1]{1,0:T(1,128)} %bitcast.6.total), custom_call_target="tpu_custom_call" | custom-call | tf_op jit(solution)/shard_map/pallas_call | solution.py:25
  37.3 0.5 broadcast.9
  37.8 0.7 reduce.3
  38.7 9.0 %shard_map.69 = (bf16[512,4096]{1,0:T(8,128)(2,1)}, f32[512,256]{1,0:T(8,128)S(1)}) custom-call(f32[512,4096]{1,0:T(8,128)} %shard_map.68.logs, s32[512,1]{1,0:T(8,128)S(1)} %reshape_reshape.8.rows, s32[1,4096]{1,0:T(1,128)S(1)} %bitcast.11, bf16[4096,256]{1,0:T(8,128)(2,1)S(1)} %copy-done.1), custom_call_target="tpu_custom_call" | custom-call | tf_op jit(solution)/shard_map/pallas_call | solution.py:25
  47.6 11.3 %all_to_all.58.parts = f32[8,64,256]{2,1,0:T(8,128)S(1)} all-to-all(f32[8,64,256]{2,1,0:T(8,128)S(1)} %bitcast.10), channel_id=1, replica_groups=mesh['z'=8,'far'=2,'core'=2,'col'=8] {'col'}, dimensions={0} | all-to-all | bytes 1048576 | tf_op jit(solution)/shard_map/all_to_all | solution.py:42
  59.0 0.8 shard_map.70
  59.8 4.1 %all-to-all-start.3 = ((f32[8,64,256]{2,1,0:T(8,128)}), f32[8,64,256]{2,1,0:T(8,128)S(1)}, u32[]{:S(2)}, u32[]{:S(2)}) async-start(f32[8,64,256]{2,1,0:T(8,128)} %shard_map.70), calls=%async_computation.3 | async-start | bytes 1048576 | tf_op jit(solution)/shard_map/all_to_all | solution.py:42
  63.9 7.6 %all-to-all-done.3 = f32[8,64,256]{2,1,0:T(8,128)S(1)} async-done(((f32[8,64,256]{2,1,0:T(8,128)}), f32[8,64,256]{2,1,0:T(8,128)S(1)}, u32[]{:S(2)}, u32[]{:S(2)}) %all-to-all-start.3) | async-done | bytes 524320 | tf_op jit(solution)/shard_map/all_to_all | solution.py:42
  71.5 3.7 %shard_map.72 = f32[2048,256]{1,0:T(8,128)S(1)} custom-call(s32[1]{0:T(128)} %bitcast.core, f32[512,256]{1,0:T(8,128)S(1)} %bitcast.7, bf16[512,4096]{1,0:T(8,128)(2,1)} %get-tuple-element.9.table), custom_call_target="tpu_custom_call" | custom-call | tf_op jit(solution)/shard_map/pallas_call | solution.py:25
  75.2 3.1 %collective-permute-start = (f32[2048,256]{1,0:T(8,128)S(1)}, f32[2048,256]{1,0:T(8,128)S(1)}, u32[]{:S(2)}, u32[]{:S(2)}) collective-permute-start(f32[2048,256]{1,0:T(8,128)S(1)} %shard_map.72), channel_id=1, source_target_pairs={{0,8},{8,0},{1,9},{9,1},{2,10},{10,2},{3,11},{11,3},{4,12},{12,4},... | collective-permute-start | bytes 6291464 | tf_op jit(solution)/shard_map/ppermute | solution.py:375
  78.3 3.7 %shard_map.71.left = f32[2048,256]{1,0:T(8,128)S(1)} custom-call(s32[1]{0:T(128)} %bitcast.core, f32[512,256]{1,0:T(8,128)S(1)} %bitcast.8, bf16[512,4096]{1,0:T(8,128)(2,1)} %get-tuple-element.9.table), custom_call_target="tpu_custom_call" | custom-call | tf_op jit(solution)/shard_map/pallas_call | solution.py:25
  82.1 2.9 %shard_map.73 = bf16[16,144,256]{2,1,0:T(8,128)(2,1)S(1)} custom-call(f32[2048,256]{1,0:T(8,128)S(1)} %shard_map.71.left, f32[2048,256]{1,0:T(8,128)S(1)} %collective-permute-done.right), custom_call_target="tpu_custom_call" | custom-call | tf_op jit(solution)/shard_map/pallas_call | solution.py:25
  85.0 41.3 %all_to_all.59.parts = bf16[16,144,256]{2,1,0:T(8,128)(2,1)S(1)} all-to-all(bf16[16,144,256]{2,1,0:T(8,128)(2,1)S(1)} %shard_map.73), channel_id=1, replica_groups=mesh['z'=8,'far'=2,'core'=2,'col'=8] {'z','far'}, dimensions={0} | all-to-all | bytes 2359296 | tf_op jit(solution)/shard_map/all_to_all | solution.py:42
  126.3 1.4 shard_map.74
  127.8 35.8 %all_to_all.60.mine = bf16[16,144,256]{2,1,0:T(8,128)(2,1)S(1)} all-to-all(bf16[16,144,256]{2,1,0:T(8,128)(2,1)S(1)} %shard_map.74), channel_id=1, replica_groups=mesh['z'=8,'far'=2,'core'=2,'col'=8] {'z','far'}, dimensions={0} | all-to-all | bytes 2359296 | tf_op jit(solution)/shard_map/all_to_all | solution.py:42
  163.6 2.2 collective-permute-start.1
  165.7 2.5 collective-permute-done.1.other
  168.2 4.3 %shard_map.75 = (f32[4096,256]{1,0:T(8,128)S(1)}, f32[8,16,256]{2,1,0:T(8,128)S(1)}) custom-call(s32[1]{0:T(128)} %bitcast.core, bf16[16,144,256]{2,1,0:T(8,128)(2,1)S(1)} %all_to_all.60.mine, bf16[16,144,256]{2,1,0:T(8,128)(2,1)S(1)} %collective-permute-done.1.other), custom_call_target="tpu_custom_call" | custom-call | tf_op jit(solution)/shard_map/pallas_call | solution.py:25
  172.6 7.9 %all_to_all.61.grams = f32[8,16,256]{2,1,0:T(8,128)S(1)} all-to-all(f32[8,16,256]{2,1,0:T(8,128)S(1)} %get-tuple-element.10), channel_id=1, replica_groups=mesh['z'=8,'far'=2,'core'=2,'col'=8] {'col'}, dimensions={0} | all-to-all | bytes 262144 | tf_op jit(solution)/shard_map/all_to_all | solution.py:42
  180.4 8.2 %shard_map.76 = (bf16[4096,256]{1,0:T(8,128)(2,1)S(1)}, f32[8,96,256]{2,1,0:T(8,128)S(1)}) custom-call(f32[8,16,256]{2,1,0:T(8,128)S(1)} %all_to_all.61.grams, f32[4096,256]{1,0:T(8,128)S(1)} %get-tuple-element.11.value, bf16[512,4096]{1,0:T(8,128)(2,1)S(1)} %copy-done), custom_call_target="tpu_custom_call" | custom-call | tf_op jit(solution)/shard_map/pallas_call | solution.py:25
  188.6 13.1 %all_to_all.62.parts = f32[8,96,256]{2,1,0:T(8,128)S(1)} all-to-all(f32[8,96,256]{2,1,0:T(8,128)S(1)} %get-tuple-element.12), channel_id=1, replica_groups=mesh['z'=8,'far'=2,'core'=2,'col'=8] {'col'}, dimensions={0} | all-to-all | bytes 1572864 | tf_op jit(solution)/shard_map/all_to_all | solution.py:42
  201.8 13.6 %all_to_all.63.packed = f32[8,96,256]{2,1,0:T(8,128)S(1)} all-to-all(f32[8,96,256]{2,1,0:T(8,128)S(1)} %shard_map.77), channel_id=1, replica_groups=mesh['z'=8,'far'=2,'core'=2,'col'=8] {'col'}, dimensions={0} | all-to-all | bytes 1572864 | tf_op jit(solution)/shard_map/all_to_all | solution.py:42
  215.4 0.7 shard_map.78
  216.1 19.3 %all_to_all.64.parts = f32[32,8,256]{2,1,0:T(8,128)S(1)} all-to-all(f32[32,8,256]{2,1,0:T(8,128)S(1)} %shard_map.78), channel_id=1, replica_groups=mesh['z'=8,'far'=2,'core'=2,'col'=8] {'z','far','core'}, dimensions={0} | all-to-all | bytes 524288 | tf_op jit(solution)/shard_map/all_to_all | solution.py:42
  235.5 0.8 shard_map.79
  236.2 4.4 %all-to-all-start.10 = ((f32[32,8,256]{2,1,0:T(8,128)}), f32[32,8,256]{2,1,0:T(8,128)S(1)}, u32[]{:S(2)}, u32[]{:S(2)}) async-start(f32[32,8,256]{2,1,0:T(8,128)} %shard_map.79), calls=%async_computation.10 | async-start | bytes 524288 | tf_op jit(solution)/shard_map/all_to_all | solution.py:42
  240.6 13.0 %shard_map.81 = f32[4096,256]{1,0:T(8,128)} custom-call(f32[8,96,256]{2,1,0:T(8,128)S(1)} %all_to_all.63.packed, bf16[4096,256]{1,0:T(8,128)(2,1)S(1)} %get-tuple-element.13.second), custom_call_target="tpu_custom_call" | custom-call | tf_op jit(solution)/shard_map/pallas_call | solution.py:25
  253.7 11.4 %shard_map.80 = f32[512,256]{1,0:T(8,128)} custom-call(f32[8,96,256]{2,1,0:T(8,128)S(1)} %all_to_all.63.packed, f32[256,256]{1,0:T(8,128)S(1)} %bitcast.9), custom_call_target="tpu_custom_call" | custom-call | tf_op jit(solution)/shard_map/pallas_call | solution.py:25
  (9 shorter events, 0.4 us)
Async XLA Ops:
  13.3 25.3 %all-to-all-start.1 = ((s32[32,1,128]{2,1,0:T(1,128)}), s32[32,1,128]{2,1,0:T(1,128)S(1)}, u32[]{:S(2)}, u32[]{:S(2)}) async-start(s32[32,1,128]{2,1,0:T(1,128)} %broadcast_in_dim.5), calls=%async_computation.1 | async-start | bytes 32768 | tf_op jit(solution)/shard_map/all_to_all | solution.py:42
  26.9 11.8 %copy-start.1 = (bf16[4096,256]{1,0:T(8,128)(2,1)S(1)}, bf16[4096,256]{1,0:T(8,128)(2,1)}, u32[]{:S(2)}) copy-start(bf16[4096,256]{1,0:T(8,128)(2,1)} %sketch.1) | copy-start | bytes 6291460
  59.8 11.7 %all-to-all-start.3 = ((f32[8,64,256]{2,1,0:T(8,128)}), f32[8,64,256]{2,1,0:T(8,128)S(1)}, u32[]{:S(2)}, u32[]{:S(2)}) async-start(f32[8,64,256]{2,1,0:T(8,128)} %shard_map.70), calls=%async_computation.3 | async-start | bytes 1048576 | tf_op jit(solution)/shard_map/all_to_all | solution.py:42
  75.2 6.9 %collective-permute-start = (f32[2048,256]{1,0:T(8,128)S(1)}, f32[2048,256]{1,0:T(8,128)S(1)}, u32[]{:S(2)}, u32[]{:S(2)}) collective-permute-start(f32[2048,256]{1,0:T(8,128)S(1)} %shard_map.72), channel_id=1, source_target_pairs={{0,8},{8,0},{1,9},{9,1},{2,10},{10,2},{3,11},{11,3},{4,12},{12,4},... | collective-permute-start | bytes 6291464 | tf_op jit(solution)/shard_map/ppermute | solution.py:375
  127.8 52.7 %copy-start = (bf16[512,4096]{1,0:T(8,128)(2,1)S(1)}, bf16[512,4096]{1,0:T(8,128)(2,1)}, u32[]{:S(2)}) copy-start(bf16[512,4096]{1,0:T(8,128)(2,1)} %get-tuple-element.9.table) | copy-start | bytes 12582916
  163.6 4.6 %collective-permute-start.1 = (bf16[16,144,256]{2,1,0:T(8,128)(2,1)S(1)}, bf16[16,144,256]{2,1,0:T(8,128)(2,1)S(1)}, u32[]{:S(2)}, u32[]{:S(2)}) collective-permute-start(bf16[16,144,256]{2,1,0:T(8,128)(2,1)S(1)} %all_to_all.60.mine), channel_id=1, source_target_pairs={{0,8},{8,0},{1,9},{9,1},{2,10},{10,2},{3,11},{11,3},{4,12},{12,4},... | collective-permute-start | bytes 3538952 | tf_op jit(solution)/shard_map/ppermute | solution.py:381
  236.2 17.4 %all-to-all-start.10 = ((f32[32,8,256]{2,1,0:T(8,128)}), f32[32,8,256]{2,1,0:T(8,128)S(1)}, u32[]{:S(2)}, u32[]{:S(2)}) async-start(f32[32,8,256]{2,1,0:T(8,128)} %shard_map.79), calls=%async_computation.10 | async-start | bytes 524288 | tf_op jit(solution)/shard_map/all_to_all | solution.py:42
